TPU v7x, 32 devices: a whole 2x2x4 slice. The times are simulated.
32 devices in a mesh: tm: 8 (over z, y), rows: 4 (over x, core).
Axes of the slice: x: 2, y: 2, z: 4, core: 2. Of those that a mesh axis runs over, the one named last changes fastest.
Arguments:
- upstream: bfloat16 [32, 32, 128, 128], P('tm', 'rows'), may hold values from -6 to 6
- saved_first: bfloat16 [32, 32, 128, 128], P('tm', 'rows'), may hold values from -8 to 8
- saved_second: bfloat16 [32, 32, 128, 128], P('tm', 'rows'), may hold values from -8 to 8
- weight_first: bfloat16 [3456, 128], replicated, may hold values from -0.109375 to 0.109375
- weight_second: bfloat16 [3456, 128], replicated, may hold values from -0.109375 to 0.109375
Outputs:
- grad_input: bfloat16 [32, 32, 128, 128], P('tm', 'rows')
- wgrad_first: float32 [3456, 128], P('tm')
- wgrad_second: float32 [3456, 128], P('tm')
All inputs are finite; a program needn't handle non-finite values.
Results may differ from a plain program's by a relative error of at most 0.005.
Values may be sent and summed in bfloat16 or wider, within the bound.
A program may use at most 64 MiB of HBM per device.

v0:
```python
import math

import jax
import jax.numpy as jnp
from jax import lax
from jax.sharding import PartitionSpec as P


def extended(cells, sides, width):
    for axis, dim in sides:
        count = lax.axis_size(axis)
        ends = count - 1
        head = lax.slice_in_dim(cells, 0, width, axis=dim)
        tail = lax.slice_in_dim(cells, cells.shape[dim] - width, cells.shape[dim], axis=dim)
        cells = jnp.concatenate(
            [
                lax.ppermute(tail, axis, [(i, (i + 1) % count) for i in range(ends)]),
                cells,
                lax.ppermute(head, axis, [((i + 1) % count, i) for i in range(ends)]),
            ],
            axis=dim,
        )
    return cells


def passed_along(block, axis, distance):
    devices = range(lax.axis_size(axis))
    route = [(i - distance, i) for i in devices if i - distance in devices]
    return lax.ppermute(block, axis, route)


def silu_slope(value):
    sigma = jax.nn.sigmoid(value)
    return sigma * (1.0 + value * (1.0 - sigma))


def extend(grad_out):
    banded_now = extended(grad_out, (("rows", 1),), 1)
    later = passed_along(banded_now[:2], "tm", -1)
    banded = jnp.concatenate([banded_now, later], axis=0)
    return jnp.pad(banded, ((0, 0), (0, 0), (1, 1), (0, 0)))


def frame_columns(padded, frame, height, width):
    slab = lax.dynamic_slice_in_dim(padded, frame, 3, 0)
    pieces = []
    for shift_t in range(3):
        for shift_r in range(3):
            for shift_c in range(3):
                pieces.append(
                    slab[
                        2 - shift_t,
                        2 - shift_r : 2 - shift_r + height,
                        2 - shift_c : 2 - shift_c + width,
                    ]
                )
    return jnp.concatenate(pieces, axis=-1).reshape(height * width, -1)


def layer_back(grad_out, saved, weight):
    frames, height, width, chans = grad_out.shape
    padded = extend(grad_out)
    flipped = weight.reshape(27, chans, chans).transpose(0, 2, 1).reshape(27 * chans, chans)

    def one_frame(total, frame):
        columns = frame_columns(padded, frame, height, width)
        spread = jnp.dot(columns, flipped, preferred_element_type=jnp.float32)
        local_saved = (
            lax.dynamic_index_in_dim(saved, frame, 0, keepdims=False)
            .reshape(height * width, chans)
            .astype(jnp.float32)
        )
        active = jax.nn.silu(local_saved).astype(jnp.bfloat16)
        total = total + lax.dot_general(
            active, columns, (((0,), (0,)), ((), ())), preferred_element_type=jnp.float32
        )
        result = (
            (spread * silu_slope(local_saved)).astype(jnp.bfloat16).reshape(height, width, chans)
        )
        return (total, result)

    start = jnp.zeros((chans, 27 * chans), jnp.float32)
    total, grads = lax.scan(one_frame, start, jnp.arange(frames, dtype=jnp.int32))
    wsum = total.reshape(chans, 27, chans).transpose(1, 0, 2).reshape(27 * chans, chans)
    return (grads, wsum)


def body(upstream, saved_first, saved_second, weight_first, weight_second):
    grad_mid, wsum_second = layer_back(upstream, saved_second, weight_second)
    grad_input, wsum_first = layer_back(grad_mid, saved_first, weight_first)
    frames, height, width, chans = upstream.shape
    factor = 1.0 / math.sqrt(frames * lax.axis_size("tm") * height * lax.axis_size("rows") * width)
    summed_first, summed_second = lax.psum((wsum_first, wsum_second), "rows")
    share_first, share_second = (
        lax.psum_scatter(summed_first, "tm", scatter_dimension=0, tiled=True),
        lax.psum_scatter(summed_second, "tm", scatter_dimension=0, tiled=True),
    )
    return (grad_input, share_first * factor, share_second * factor)


def solution(mesh):
    return jax.shard_map(
        body,
        mesh=mesh,
        in_specs=(
            P("tm", "rows", None, None),
            P("tm", "rows", None, None),
            P("tm", "rows", None, None),
            P(),
            P(),
        ),
        out_specs=(P("tm", "rows", None, None), P("tm", None), P("tm", None)),
        check_vma=False,
    )
```

profile of v0, /device:TPU:0, one launch (start us, length us, event | category | flops | bytes accessed | tf_op | source)
XLA Modules:
  0.0 346.3 jit_solution(1226086394219848578)
XLA Ops:
  19.5 13.5 %collective-permute-done.2 = bf16[2,10,128,128]{3,2,1,0:T(8,128)(2,1)} collective-permute-done((bf16[2,10,128,128]{3,2,1,0:T(8,128)(2,1)S(1)}, bf16[2,10,128,128]{3,2,1,0:T(8,128)(2,1)}, u32[]{:S(2)}, u32[]{:S(2)}) %collective-permute-start.2) | collective-permute-done | bytes 655392 | tf_op jit(solution)/shard_map/ppermute | solution.py:29
  35.3 81.7 %while.26 = (s32[]{:T(128)}, f32[128,3456]{1,0:T(8,128)}, bf16[4,8,128,128]{3,2,1,0:T(8,128)(2,1)S(1)}, s32[4]{0:T(128)S(1)}, bf16[4,8,128,128]{3,2,1,0:T(8,128)...) while((s32[]{:T(128)}, f32[128,3456]{1,0:T(8,128)}, ...), condition=%wide.region_1.2_spmd.clone, body=%wide.region_0.1_spmd.clone.sunk | while | flops 1814921216 | bytes 80576848 | solution.py:83
  39.1 3.8 %constant_dynamic-slice_fusion.58 = (bf16[1,8,128,128]{3,2,1,0:T(8,128)(2,1)S(1)}, bf16[1,8,128,128]{3,2,1,0:T(8,128)(2,1)S(1)}, bf16[1,8,128,128]{3,2,1,0:T(8,1...) fusion(bf16[6,10,130,128]{3,2,1,0:T(8,128)(2,1)S(1)} %get-tuple, ...), kind=kLoop, calls=%fused_computation.67.clone.1 | loop fusion | bytes 14680088 | tf_op jit(solution)/shard_map/while/body/eval_jaxpr/slice | solution.py:51
  44.9 2.9 copy-done
  49.9 5.5 %convolution_add_fusion.4 = f32[128,3456]{1,0:T(8,128)} fusion(bf16[1024,3456]{1,0:T(8,128)(2,1)} %copy-done, f32[128,3456]{1,0:T(8,128)} %get-tuple-element.435, pred[]{:T(512)S(6)} %compare.42, bf16[1024,128]{1,0:T(8,128)(2,1)S(1)} %bitcast.217), kind=kOutput, calls=%fused_computation.clone.1 | convolution fusion | flops 907640832 | bytes 10878977 | tf_op jit(solution)/shard_map/while/body/eval_jaxpr/dot_general | solution.py:74
  59.2 3.8 %constant_dynamic-slice_fusion.58 = (bf16[1,8,128,128]{3,2,1,0:T(8,128)(2,1)S(1)}, bf16[1,8,128,128]{3,2,1,0:T(8,128)(2,1)S(1)}, bf16[1,8,128,128]{3,2,1,0:T(8,1...) fusion(bf16[6,10,130,128]{3,2,1,0:T(8,128)(2,1)S(1)} %get-tuple, ...), kind=kLoop, calls=%fused_computation.67.clone.1 | loop fusion | bytes 14680088 | tf_op jit(solution)/shard_map/while/body/eval_jaxpr/slice | solution.py:51
  69.9 6.0 %convolution_add_fusion.4 = f32[128,3456]{1,0:T(8,128)} fusion(bf16[1024,3456]{1,0:T(8,128)(2,1)} %copy-done, f32[128,3456]{1,0:T(8,128)} %get-tuple-element.435, pred[]{:T(512)S(6)} %compare.42, bf16[1024,128]{1,0:T(8,128)(2,1)S(1)} %bitcast.217), kind=kOutput, calls=%fused_computation.clone.1 | convolution fusion | flops 907640832 | bytes 10878977 | tf_op jit(solution)/shard_map/while/body/eval_jaxpr/dot_general | solution.py:74
  79.8 3.8 %constant_dynamic-slice_fusion.58 = (bf16[1,8,128,128]{3,2,1,0:T(8,128)(2,1)S(1)}, bf16[1,8,128,128]{3,2,1,0:T(8,128)(2,1)S(1)}, bf16[1,8,128,128]{3,2,1,0:T(8,1...) fusion(bf16[6,10,130,128]{3,2,1,0:T(8,128)(2,1)S(1)} %get-tuple, ...), kind=kLoop, calls=%fused_computation.67.clone.1 | loop fusion | bytes 14680088 | tf_op jit(solution)/shard_map/while/body/eval_jaxpr/slice | solution.py:51
  90.5 6.0 %convolution_add_fusion.4 = f32[128,3456]{1,0:T(8,128)} fusion(bf16[1024,3456]{1,0:T(8,128)(2,1)} %copy-done, f32[128,3456]{1,0:T(8,128)} %get-tuple-element.435, pred[]{:T(512)S(6)} %compare.42, bf16[1024,128]{1,0:T(8,128)(2,1)S(1)} %bitcast.217), kind=kOutput, calls=%fused_computation.clone.1 | convolution fusion | flops 907640832 | bytes 10878977 | tf_op jit(solution)/shard_map/while/body/eval_jaxpr/dot_general | solution.py:74
  100.3 3.8 %constant_dynamic-slice_fusion.58 = (bf16[1,8,128,128]{3,2,1,0:T(8,128)(2,1)S(1)}, bf16[1,8,128,128]{3,2,1,0:T(8,128)(2,1)S(1)}, bf16[1,8,128,128]{3,2,1,0:T(8,1...) fusion(bf16[6,10,130,128]{3,2,1,0:T(8,128)(2,1)S(1)} %get-tuple, ...), kind=kLoop, calls=%fused_computation.67.clone.1 | loop fusion | bytes 14680088 | tf_op jit(solution)/shard_map/while/body/eval_jaxpr/slice | solution.py:51
  111.0 6.0 %convolution_add_fusion.4 = f32[128,3456]{1,0:T(8,128)} fusion(bf16[1024,3456]{1,0:T(8,128)(2,1)} %copy-done, f32[128,3456]{1,0:T(8,128)} %get-tuple-element.435, pred[]{:T(512)S(6)} %compare.42, bf16[1024,128]{1,0:T(8,128)(2,1)S(1)} %bitcast.217), kind=kOutput, calls=%fused_computation.clone.1 | convolution fusion | flops 907640832 | bytes 10878977 | tf_op jit(solution)/shard_map/while/body/eval_jaxpr/dot_general | solution.py:74
  117.0 4.4 %collective-permute-start.3 = (bf16[4,1,128,128]{3,2,1,0:T(8,128)(2,1)S(1)}, bf16[4,1,128,128]{3,2,1,0:T(8,128)(2,1)S(1)}, u32[]{:S(2)}, u32[]{:S(2)}) collective-permute-start(bf16[4,1,128,128]{3,2,1,0:T(8,128)(2,1)S(1)} %get-tuple-element.218), channel_id=1, source_target_pairs={{0,1},{1,2},{2,3},{4,5},{5,6},{6,7},{8,9},{9,10},{10,11},{12,13},{... | collective-permute-start | bytes 393224 | tf_op jit(solution)/shard_map/ppermute | solution.py:17
  133.6 10.6 %collective-permute-done.5 = bf16[2,10,128,128]{3,2,1,0:T(8,128)(2,1)} collective-permute-done((bf16[2,10,128,128]{3,2,1,0:T(8,128)(2,1)}, bf16[2,10,128,128]{3,2,1,0:T(8,128)(2,1)}, u32[]{:S(2)}, u32[]{:S(2)}) %collective-permute-start.5) | collective-permute-done | bytes 655392 | tf_op jit(solution)/shard_map/ppermute | solution.py:29
  146.8 81.6 %while.27 = (s32[]{:T(128)}, f32[128,3456]{1,0:T(8,128)}, bf16[4,8,128,128]{3,2,1,0:T(8,128)(2,1)S(1)}, s32[4]{0:T(128)S(1)}, bf16[4,8,128,128]{3,2,1,0:T(8,128)...) while((s32[]{:T(128)}, f32[128,3456]{1,0:T(8,128)}, ...), condition=%wide.region_3.4_spmd.clone, body=%wide.region_2.3_spmd.clone.sunk | while | flops 1814921216 | bytes 80576848 | solution.py:83
  150.6 3.8 %constant_dynamic-slice_fusion.59 = (bf16[1,8,128,128]{3,2,1,0:T(8,128)(2,1)S(1)}, bf16[1,8,128,128]{3,2,1,0:T(8,128)(2,1)S(1)}, bf16[1,8,128,128]{3,2,1,0:T(8,1...) fusion(bf16[6,10,130,128]{3,2,1,0:T(8,128)(2,1)S(1)} %get-tuple, ...), kind=kLoop, calls=%fused_computation.137.clone.1 | loop fusion | bytes 14680088 | tf_op jit(solution)/shard_map/while/body/eval_jaxpr/slice | solution.py:51
  161.4 5.5 %convolution_add_fusion.5 = f32[128,3456]{1,0:T(8,128)} fusion(bf16[1024,3456]{1,0:T(8,128)(2,1)} %copy-done.1, f32[128,3456]{1,0:T(8,128)} %get-tuple-element.474, pred[]{:T(512)S(6)} %compare.43, bf16[1024,128]{1,0:T(8,128)(2,1)S(1)} %bitcast.219), kind=kOutput, calls=%fused_computation.70.clone.1 | convolution fusion | flops 907640832 | bytes 10878977 | tf_op jit(solution)/shard_map/while/body/eval_jaxpr/dot_general | solution.py:74
  170.7 3.8 %constant_dynamic-slice_fusion.59 = (bf16[1,8,128,128]{3,2,1,0:T(8,128)(2,1)S(1)}, bf16[1,8,128,128]{3,2,1,0:T(8,128)(2,1)S(1)}, bf16[1,8,128,128]{3,2,1,0:T(8,1...) fusion(bf16[6,10,130,128]{3,2,1,0:T(8,128)(2,1)S(1)} %get-tuple, ...), kind=kLoop, calls=%fused_computation.137.clone.1 | loop fusion | bytes 14680088 | tf_op jit(solution)/shard_map/while/body/eval_jaxpr/slice | solution.py:51
  181.4 6.0 %convolution_add_fusion.5 = f32[128,3456]{1,0:T(8,128)} fusion(bf16[1024,3456]{1,0:T(8,128)(2,1)} %copy-done.1, f32[128,3456]{1,0:T(8,128)} %get-tuple-element.474, pred[]{:T(512)S(6)} %compare.43, bf16[1024,128]{1,0:T(8,128)(2,1)S(1)} %bitcast.219), kind=kOutput, calls=%fused_computation.70.clone.1 | convolution fusion | flops 907640832 | bytes 10878977 | tf_op jit(solution)/shard_map/while/body/eval_jaxpr/dot_general | solution.py:74
  191.2 3.8 %constant_dynamic-slice_fusion.59 = (bf16[1,8,128,128]{3,2,1,0:T(8,128)(2,1)S(1)}, bf16[1,8,128,128]{3,2,1,0:T(8,128)(2,1)S(1)}, bf16[1,8,128,128]{3,2,1,0:T(8,1...) fusion(bf16[6,10,130,128]{3,2,1,0:T(8,128)(2,1)S(1)} %get-tuple, ...), kind=kLoop, calls=%fused_computation.137.clone.1 | loop fusion | bytes 14680088 | tf_op jit(solution)/shard_map/while/body/eval_jaxpr/slice | solution.py:51
  202.0 6.0 %convolution_add_fusion.5 = f32[128,3456]{1,0:T(8,128)} fusion(bf16[1024,3456]{1,0:T(8,128)(2,1)} %copy-done.1, f32[128,3456]{1,0:T(8,128)} %get-tuple-element.474, pred[]{:T(512)S(6)} %compare.43, bf16[1024,128]{1,0:T(8,128)(2,1)S(1)} %bitcast.219), kind=kOutput, calls=%fused_computation.70.clone.1 | convolution fusion | flops 907640832 | bytes 10878977 | tf_op jit(solution)/shard_map/while/body/eval_jaxpr/dot_general | solution.py:74
  211.7 3.8 %constant_dynamic-slice_fusion.59 = (bf16[1,8,128,128]{3,2,1,0:T(8,128)(2,1)S(1)}, bf16[1,8,128,128]{3,2,1,0:T(8,128)(2,1)S(1)}, bf16[1,8,128,128]{3,2,1,0:T(8,1...) fusion(bf16[6,10,130,128]{3,2,1,0:T(8,128)(2,1)S(1)} %get-tuple, ...), kind=kLoop, calls=%fused_computation.137.clone.1 | loop fusion | bytes 14680088 | tf_op jit(solution)/shard_map/while/body/eval_jaxpr/slice | solution.py:51
  222.5 5.9 %convolution_add_fusion.5 = f32[128,3456]{1,0:T(8,128)} fusion(bf16[1024,3456]{1,0:T(8,128)(2,1)} %copy-done.1, f32[128,3456]{1,0:T(8,128)} %get-tuple-element.474, pred[]{:T(512)S(6)} %compare.43, bf16[1024,128]{1,0:T(8,128)(2,1)S(1)} %bitcast.219), kind=kOutput, calls=%fused_computation.70.clone.1 | convolution fusion | flops 907640832 | bytes 10878977 | tf_op jit(solution)/shard_map/while/body/eval_jaxpr/dot_general | solution.py:74
  233.0 70.8 %reduce-scatter.3.cloned.1.call-done = f32[432,128]{1,0:T(8,128)} async-done(((f32[3456,128]{1,0:T(8,128)}), f32[432,128]{1,0:T(8,128)}) %reduce-scatter.3.cloned.1.call-update) | async-done | bytes 221200 | tf_op jit(solution)/shard_map/reduce_scatter | solution.py:95
  303.9 34.1 %all-reduce.5.cloned.1.call-done = (f32[432,128]{1,0:T(8,128)}, f32[432,128]{1,0:T(8,128)}) async-done(((f32[432,128]{1,0:T(8,128)}, f32[432,128]{1,0:T(8,128)}), (f32[432,128]{1,0:T(8,128)}, f32[432,128]{1,0:T(8,128)})) %all-reduce.5.cloned.1.call-update) | async-done | bytes 442384 | tf_op jit(solution)/shard_map/psum | solution.py:93
  (318 shorter events, 90.7 us)
Async XLA Ops:
  7.2 225.9 %reduce-scatter.5.cloned.1.call-start = ((), (), s32[]{:S(2)}) async-start(), calls=%async_computation.3 | async-start | bytes 1990656 | tf_op jit(solution)/shard_map/reduce_scatter | solution.py:96
  8.2 3.7 %collective-permute-start = (bf16[4,1,128,128]{3,2,1,0:T(8,128)(2,1)S(1)}, bf16[4,1,128,128]{3,2,1,0:T(8,128)(2,1)S(1)}, u32[]{:S(2)}, u32[]{:S(2)}) collective-permute-start(bf16[4,1,128,128]{3,2,1,0:T(8,128)(2,1)S(1)} %get-tuple-element.220), channel_id=1, source_target_pairs={{0,1},{1,2},{2,3},{4,5},{5,6},{6,7},{8,9},{9,10},{10,11},{12,13},{... | collective-permute-start | bytes 393224 | tf_op jit(solution)/shard_map/ppermute | solution.py:17
  10.6 5.3 %collective-permute-start.1 = (bf16[4,1,128,128]{3,2,1,0:T(8,128)(2,1)S(1)}, bf16[4,1,128,128]{3,2,1,0:T(8,128)(2,1)S(1)}, u32[]{:S(2)}, u32[]{:S(2)}) collective-permute-start(bf16[4,1,128,128]{3,2,1,0:T(8,128)(2,1)S(1)} %get-tuple-element.219), channel_id=1, source_target_pairs={{1,0},{2,1},{3,2},{5,4},{6,5},{7,6},{9,8},{10,9},{11,10},{13,12},{... | collective-permute-start | bytes 393224 | tf_op jit(solution)/shard_map/ppermute | solution.py:19
  16.0 17.0 %collective-permute-start.2 = (bf16[2,10,128,128]{3,2,1,0:T(8,128)(2,1)S(1)}, bf16[2,10,128,128]{3,2,1,0:T(8,128)(2,1)}, u32[]{:S(2)}, u32[]{:S(2)}) collective-permute-start(bf16[2,10,128,128]{3,2,1,0:T(8,128)(2,1)S(1)} %slice.240), channel_id=1, source_target_pairs={{4,0},{8,4},{12,8},{16,12},{20,16},{24,20},{28,24},{5,1},{9,5},{13... | collective-permute-start | bytes 1966088 | tf_op jit(solution)/shard_map/ppermute | solution.py:29
  43.0 4.8 %copy-start.6 = (bf16[3456,128]{1,0:T(8,128)(2,1)S(1)}, bf16[3456,128]{1,0:T(8,128)(2,1)}, u32[]{:S(2)}) copy-start(bf16[3456,128]{1,0:T(8,128)(2,1)} %get-tuple-element.453) | copy-start | bytes 2654212 | tf_op jit(solution)/shard_map/while
  44.9 2.9 copy-start
  63.0 4.8 %copy-start.6 = (bf16[3456,128]{1,0:T(8,128)(2,1)S(1)}, bf16[3456,128]{1,0:T(8,128)(2,1)}, u32[]{:S(2)}) copy-start(bf16[3456,128]{1,0:T(8,128)(2,1)} %get-tuple-element.453) | copy-start | bytes 2654212 | tf_op jit(solution)/shard_map/while
  65.0 2.9 copy-start
  83.6 4.8 %copy-start.6 = (bf16[3456,128]{1,0:T(8,128)(2,1)S(1)}, bf16[3456,128]{1,0:T(8,128)(2,1)}, u32[]{:S(2)}) copy-start(bf16[3456,128]{1,0:T(8,128)(2,1)} %get-tuple-element.453) | copy-start | bytes 2654212 | tf_op jit(solution)/shard_map/while
  85.5 2.9 copy-start
  104.1 4.8 %copy-start.6 = (bf16[3456,128]{1,0:T(8,128)(2,1)S(1)}, bf16[3456,128]{1,0:T(8,128)(2,1)}, u32[]{:S(2)}) copy-start(bf16[3456,128]{1,0:T(8,128)(2,1)} %get-tuple-element.453) | copy-start | bytes 2654212 | tf_op jit(solution)/shard_map/while
  106.1 2.9 copy-start
  117.0 13.2 %copy-start.2 = (f32[128,3456]{1,0:T(8,128)S(1)}, f32[128,3456]{1,0:T(8,128)}, u32[]{:S(2)}) copy-start(f32[128,3456]{1,0:T(8,128)} %get-tuple-element.82) | copy-start | bytes 5308420
  117.0 5.8 %collective-permute-start.3 = (bf16[4,1,128,128]{3,2,1,0:T(8,128)(2,1)S(1)}, bf16[4,1,128,128]{3,2,1,0:T(8,128)(2,1)S(1)}, u32[]{:S(2)}, u32[]{:S(2)}) collective-permute-start(bf16[4,1,128,128]{3,2,1,0:T(8,128)(2,1)S(1)} %get-tuple-element.218), channel_id=1, source_target_pairs={{0,1},{1,2},{2,3},{4,5},{5,6},{6,7},{8,9},{9,10},{10,11},{12,13},{... | collective-permute-start | bytes 393224 | tf_op jit(solution)/shard_map/ppermute | solution.py:17
  121.5 3.2 collective-permute-start.4
  126.7 17.5 %collective-permute-start.5 = (bf16[2,10,128,128]{3,2,1,0:T(8,128)(2,1)}, bf16[2,10,128,128]{3,2,1,0:T(8,128)(2,1)}, u32[]{:S(2)}, u32[]{:S(2)}) collective-permute-start(bf16[2,10,128,128]{3,2,1,0:T(8,128)(2,1)} %slice.241), channel_id=1, source_target_pairs={{4,0},{8,4},{12,8},{16,12},{20,16},{24,20},{28,24},{5,1},{9,5},{13... | collective-permute-start | bytes 1966088 | tf_op jit(solution)/shard_map/ppermute | solution.py:29
  133.4 170.4 %reduce-scatter.3.cloned.1.call-start = ((), (), s32[]{:S(2)}) async-start(), calls=%async_computation.2 | async-start | bytes 1990656 | tf_op jit(solution)/shard_map/reduce_scatter | solution.py:95
  154.5 4.8 %copy-start.5 = (bf16[3456,128]{1,0:T(8,128)(2,1)S(1)}, bf16[3456,128]{1,0:T(8,128)(2,1)}, u32[]{:S(2)}) copy-start(bf16[3456,128]{1,0:T(8,128)(2,1)} %get-tuple-element.492) | copy-start | bytes 2654212 | tf_op jit(solution)/shard_map/while
  174.5 4.8 %copy-start.5 = (bf16[3456,128]{1,0:T(8,128)(2,1)S(1)}, bf16[3456,128]{1,0:T(8,128)(2,1)}, u32[]{:S(2)}) copy-start(bf16[3456,128]{1,0:T(8,128)(2,1)} %get-tuple-element.492) | copy-start | bytes 2654212 | tf_op jit(solution)/shard_map/while
  195.0 4.8 %copy-start.5 = (bf16[3456,128]{1,0:T(8,128)(2,1)S(1)}, bf16[3456,128]{1,0:T(8,128)(2,1)}, u32[]{:S(2)}) copy-start(bf16[3456,128]{1,0:T(8,128)(2,1)} %get-tuple-element.492) | copy-start | bytes 2654212 | tf_op jit(solution)/shard_map/while
  197.0 2.9 copy-start.1
  215.6 4.8 %copy-start.5 = (bf16[3456,128]{1,0:T(8,128)(2,1)S(1)}, bf16[3456,128]{1,0:T(8,128)(2,1)}, u32[]{:S(2)}) copy-start(bf16[3456,128]{1,0:T(8,128)(2,1)} %get-tuple-element.492) | copy-start | bytes 2654212 | tf_op jit(solution)/shard_map/while
  228.4 111.4 %copy-start.4 = (bf16[4,8,128,128]{3,2,1,0:T(8,128)(2,1)}, bf16[4,8,128,128]{3,2,1,0:T(8,128)(2,1)S(1)}, u32[]{:S(2)}) copy-start(bf16[4,8,128,128]{3,2,1,0:T(8,128)(2,1)S(1)} %get-tuple-element.76) | copy-start | bytes 3145732
  232.9 105.0 %all-reduce.5.cloned.1.call-start = ((), (), s32[]{:S(2)}) async-start(), calls=%async_computation.4 | async-start | bytes 884736 | tf_op jit(solution)/shard_map/psum | solution.py:93
  (4 other events, 9.7 us)
Sparse Core Ops, SparseCore 0:
  133.5 71.6 reduce-scatter.4
  233.1 70.7 reduce-scatter.2
  306.4 31.5 all-reduce.4
where the time goes:
time: 348 us; the launch traced here: 346 us
  waiting for transfers between devices  133 us (38%)
  local copies, waits for them, and re-layouts  89.5 us (26%)
  matrix products  63 us (18%)
  loops' own time  28 us (8%)
  between operations  14 us (4%)
  starting transfers between devices  12.3 us (4%)
  other arithmetic  6.19 us (2%)
    reduce_scatter x1, waiting for transfers between devices, body(): lax.psum_scatter(summed_first, 'tm', scatter_dimension=0, tiled=True)  70.8 us
    dot_general x8, matrix products, one_frame(): lax.dot_general(active, columns, (((0,), (0,)), ((), ())), preferred_elem...  46.8 us
    while x240, local copies, waits for them, and re-layouts  36.2 us
    psum x1, waiting for transfers between devices, body(): summed_first, summed_second = lax.psum((wsum_first, wsum_second), 'rows')  34.1 us
    slice x8, local copies, waits for them, and re-layouts, frame_columns(): slab[2 - shift_t, 2 - shift_r:2 - shift_r + height, 2 - shift_c:2 - shift...  30.6 us
    another operation x2, loops' own time, layer_back(): lax.scan(one_frame, start, jnp.arange(frames, dtype=jnp.int32))  28 us
    ppermute x2, waiting for transfers between devices, passed_along(): return lax.ppermute(block, axis, route)  24.1 us
    dot_general x8, matrix products, one_frame(): spread = jnp.dot(columns, flipped, preferred_element_type=jnp.float32)  16.2 us
  transfers between devices with their start and end apart: 9, of which 6 were waited for; matrix products, arithmetic and copies ran while one was open for 21% of the time, Pallas kernels for 0%

commit v1 on v0

v1 whole, which is shorter than its diff:
```python
import functools
import math

import jax
import jax.numpy as jnp
from jax import lax
from jax.experimental import pallas as pl
from jax.experimental.pallas import tpu as pltpu
from jax.sharding import PartitionSpec as P

F32, BF16 = jnp.float32, jnp.bfloat16
VMEM_LIMIT = 60 * 1024 * 1024


def shifted(block, axis, step):
    count = lax.axis_size(axis)
    route = [(i - step, i) for i in range(count) if 0 <= i - step < count]
    return lax.ppermute(block, axis, route)


def halos(grad):
    height = grad.shape[1]
    above = shifted(grad[:, height - 1 :], "rows", 1)
    below = shifted(grad[:, :1], "rows", -1)
    later = shifted(grad[:2], "tm", -1)
    later_edges = shifted(jnp.concatenate([above[:2], below[:2]], axis=1), "tm", -1)
    return above, below, later, later_edges


def fill_row(cols, value, frame, row, height, width, chans):
    wide = value.astype(F32)
    place = lax.broadcasted_iota(jnp.int32, (width, chans), 0)
    after = jnp.where(place == width - 1, 0.0, pltpu.roll(wide, width - 1, 0)).astype(BF16)
    before = jnp.where(place == 0, 0.0, pltpu.roll(wide, 1, 0)).astype(BF16)
    for q in range(3):
        out_row = row - 1 + q
        if not 0 <= out_row < height:
            continue
        base = (frame * 9 + q * 3) * chans
        lines = pl.ds(out_row * width, width)
        cols[lines, pl.ds(base, chans)] = after
        cols[lines, pl.ds(base + chans, chans)] = value
        cols[lines, pl.ds(base + 2 * chans, chans)] = before


def fill(cols, grad_ref, above_ref, below_ref, later_ref, edges_ref):
    frames, height, width, chans = grad_ref.shape
    put = functools.partial(fill_row, cols, height=height, width=width, chans=chans)
    for frame in range(frames + 2):
        late = frame - frames
        if late < 0:
            first, last = above_ref[frame, 0], below_ref[frame, 0]
        else:
            first, last = edges_ref[late, 0], edges_ref[late, 1]
        put(first, frame, -1)
        put(last, frame, height)
        for row in range(height):
            put(grad_ref[frame, row] if late < 0 else later_ref[late, row], frame, row)


def spread_kernel(grad_ref, above_ref, below_ref, later_ref, edges_ref, saved_ref, weight_ref, out_ref, cols, kernels):
    frames, height, width, chans = grad_ref.shape
    span = 9 * chans
    for half in range(2):
        for j in range(4):
            p = 2 + half - j
            for tap in range(9):
                block = (
                    weight_ref[pl.ds((9 * p + tap) * chans, chans), :]
                    if 0 <= p < 3
                    else jnp.zeros((chans, chans), BF16)
                )
                kernels[pl.ds(half * chans, chans), pl.ds(j * span + tap * chans, chans)] = block
    fill(cols, grad_ref, above_ref, below_ref, later_ref, edges_ref)
    step_rows = math.gcd(4, height)
    lines = step_rows * width
    for pair in range(frames // 2):

        def chunk(index, carry, pair=pair):
            part = cols[pl.ds(pl.multiple_of(index * lines, lines), lines), pl.ds(pair * 2 * span, 4 * span)]
            spread = lax.dot_general(part, kernels[...], (((1,), (1,)), ((), ())), preferred_element_type=F32)
            for half in range(2):
                rows = pl.ds(index * step_rows, step_rows)
                value = saved_ref[2 * pair + half, rows].reshape(lines, chans).astype(F32)
                sigma = jax.nn.sigmoid(value)
                slope = sigma * (1.0 + value * (1.0 - sigma))
                result = spread[:, half * chans : (half + 1) * chans] * slope
                out_ref[2 * pair + half, rows] = result.astype(BF16).reshape(step_rows, width, chans)
            return carry

        lax.fori_loop(0, height // step_rows, chunk, 0)


def wsum_kernel(grad_ref, above_ref, below_ref, later_ref, edges_ref, saved_ref, out_ref, cols, active):
    frames, height, width, chans = grad_ref.shape
    span = 9 * chans
    fill(cols, grad_ref, above_ref, below_ref, later_ref, edges_ref)
    for frame in range(frames):
        for row in range(height):
            value = saved_ref[frame, row].astype(F32)
            act = value * jax.nn.sigmoid(value)
            active[pl.ds(frame * chans, chans), pl.ds(row * width, width)] = act.T.astype(BF16)
    out_ref[...] = jnp.zeros_like(out_ref)
    for frame in range(frames + 2):
        low, high = max(0, frame - 2), min(frames, frame + 1)
        acts = active[pl.ds(low * chans, (high - low) * chans), :]
        for q in range(3):
            part = cols[:, pl.ds(frame * span + q * 3 * chans, 3 * chans)]
            total = jnp.dot(acts, part, preferred_element_type=F32)
            for s in range(low, high):
                p = s + 2 - frame
                for k in range(3):
                    rows = pl.ds((9 * p + 3 * q + k) * chans, chans)
                    out_ref[rows, :] += total[(s - low) * chans : (s - low + 1) * chans, k * chans : (k + 1) * chans]


def vmem(count):
    return [pl.BlockSpec(memory_space=pltpu.VMEM)] * count


def spread_of(pieces, saved, weight):
    frames, height, width, chans = saved.shape
    flops = 2 * frames * height * width * 36 * chans * chans
    return pl.pallas_call(
        spread_kernel,
        out_shape=jax.ShapeDtypeStruct(saved.shape, BF16),
        in_specs=vmem(7),
        out_specs=pl.BlockSpec(memory_space=pltpu.VMEM),
        scratch_shapes=[
            pltpu.VMEM((height * width, (frames + 2) * 9 * chans), BF16),
            pltpu.VMEM((2 * chans, 36 * chans), BF16),
        ],
        compiler_params=pltpu.CompilerParams(vmem_limit_bytes=VMEM_LIMIT),
        cost_estimate=pl.CostEstimate(flops=flops, bytes_accessed=4 * saved.size, transcendentals=0),
        name="spread",
    )(*pieces, saved, weight)


def wsum_of(pieces, saved):
    frames, height, width, chans = saved.shape
    flops = 2 * frames * height * width * 27 * chans * chans
    return pl.pallas_call(
        wsum_kernel,
        out_shape=jax.ShapeDtypeStruct((27 * chans, chans), F32),
        in_specs=vmem(6),
        out_specs=pl.BlockSpec(memory_space=pltpu.VMEM),
        scratch_shapes=[
            pltpu.VMEM((height * width, (frames + 2) * 9 * chans), BF16),
            pltpu.VMEM((frames * chans, height * width), BF16),
        ],
        compiler_params=pltpu.CompilerParams(vmem_limit_bytes=VMEM_LIMIT),
        cost_estimate=pl.CostEstimate(flops=flops, bytes_accessed=4 * saved.size, transcendentals=0),
        name="wsum",
    )(*pieces, saved)


def reduced(wsum):
    depth, chans = wsum.shape
    slots, bands = lax.axis_size("tm"), lax.axis_size("rows")
    share = depth // slots
    if share % bands:
        return lax.psum_scatter(lax.psum(wsum, "rows"), "tm", scatter_dimension=0, tiled=True)
    parts = wsum.reshape(slots, bands, share // bands, chans)
    banded = lax.psum_scatter(parts, "rows", scatter_dimension=1, tiled=True)
    mine = lax.psum_scatter(banded, "tm", scatter_dimension=0, tiled=True)
    return lax.all_gather(mine.reshape(share // bands, chans), "rows", axis=0, tiled=True)


def body(upstream, saved_first, saved_second, weight_first, weight_second):
    pieces = (upstream, *halos(upstream))
    grad_mid = spread_of(pieces, saved_second, weight_second)
    pieces_mid = (grad_mid, *halos(grad_mid))
    wsum_second = wsum_of(pieces, saved_second)
    grad_input = spread_of(pieces_mid, saved_first, weight_first)
    wsum_first = wsum_of(pieces_mid, saved_first)
    frames, height, width, chans = upstream.shape
    factor = 1.0 / math.sqrt(frames * lax.axis_size("tm") * height * lax.axis_size("rows") * width)
    return (grad_input, reduced(wsum_first) * factor, reduced(wsum_second) * factor)


def solution(mesh):
    grid = P("tm", "rows", None, None)
    return jax.shard_map(
        body,
        mesh=mesh,
        in_specs=(grid, grid, grid, P(), P()),
        out_specs=(grid, P("tm", None), P("tm", None)),
        check_vma=False,
    )
```

time: 348 us -> 226 us (0.65)
  local copies, waits for them, and re-layouts: 89.5 us -> 18.4 us
  matrix products: 63 us -> 0 us
  Pallas kernels: 0 us -> 40.5 us
  loops' own time: 28 us -> 0 us
  blocking collectives: 0 us -> 11.3 us
  waiting for transfers between devices: 133 us -> 125 us
  other arithmetic: 6.19 us -> 1.86 us
    unnamed x3 -> x4, waiting for transfers between devices: 0.05 us -> 68.2 us
    dot_general x16 -> x0, matrix products: 63 us -> none  [the longest x8 46.8 us: one_frame(): lax.dot_general(active, columns, (((0,), (0,)), ((), ())), preferred_elem...]
    pallas_call x0 -> x4, Pallas kernels: none -> 40.5 us  [the longest x2 22.3 us: spread_of(): pl.pallas_call(spread_kernel, out_shape=jax.ShapeDtypeStruct(saved.shape,...]
    while x242 -> x0, local copies, waits for them, and re-layouts: 39.9 us -> none
    reduce_scatter x2, waiting for transfers between devices: 70.8 us -> 35.5 us  [reduced(): banded = lax.psum_scatter(parts, 'rows', scatter_dimension=1, tiled=True)]
    psum x1 -> x0, waiting for transfers between devices: 34.1 us -> none  [body(): summed_first, summed_second = lax.psum((wsum_first, wsum_second), 'rows')]
    slice x12 -> x8, local copies, waits for them, and re-layouts: 32.5 us -> 4.16 us  [the longest x2 2.15 us: halos(): later = shifted(grad[:2], 'tm', -1)]
    another operation x2 -> x0, loops' own time: 28 us -> none  [layer_back(): lax.scan(one_frame, start, jnp.arange(frames, dtype=jnp.int32))]
  transfers between devices with their start and end apart: 9 -> 11, of which waited for: 6 -> 6; matrix products, arithmetic and copies ran while one was open for 21% -> 3% of each run, Pallas kernels for 0% -> 14%
where the time goes in v1:
time: 226 us; the launch traced here: 225 us
  waiting for transfers between devices  125 us (55%)
  Pallas kernels  40.5 us (18%)
  local copies, waits for them, and re-layouts  18.4 us (8%)
  starting transfers between devices  14.1 us (6%)
  between operations  14 us (6%)
  blocking collectives  11.3 us (5%)
    unnamed x4, waiting for transfers between devices  68.2 us
    reduce_scatter x2, waiting for transfers between devices, reduced(): banded = lax.psum_scatter(parts, 'rows', scatter_dimension=1, tiled=True)  35.5 us
    pallas_call x2, Pallas kernels, spread_of(): pl.pallas_call(spread_kernel, out_shape=jax.ShapeDtypeStruct(saved.shape,...  22.3 us
    ppermute x8, waiting for transfers between devices, shifted(): return lax.ppermute(block, axis, route)  21.3 us
    pallas_call x2, Pallas kernels, wsum_of(): pl.pallas_call(wsum_kernel, out_shape=jax.ShapeDtypeStruct((27 * chans, c...  18.2 us
    ppermute x8, starting transfers between devices, shifted(): return lax.ppermute(block, axis, route)  14 us
    all_gather x2, blocking collectives, reduced(): lax.all_gather(mine.reshape(share // bands, chans), 'rows', axis=0, tiled...  11.3 us
    reshape x4, local copies, waits for them, and re-layouts, reduced(): parts = wsum.reshape(slots, bands, share // bands, chans)  7.5 us
  transfers between devices with their start and end apart: 11, of which 6 were waited for; matrix products, arithmetic and copies ran while one was open for 3% of the time, Pallas kernels for 14%

profile of v1, /device:TPU:0, one launch (start us, length us, event | category | flops | bytes accessed | tf_op | source)
XLA Modules:
  0.0 225.1 jit_solution(6860968367624802199)
XLA Ops:
  8.3 1.3 collective-permute-start.2
  10.6 1.3 collective-permute-start.1
  11.9 3.0 %collective-permute-start = (bf16[4,1,128,128]{3,2,1,0:T(8,128)(2,1)S(1)}, bf16[4,1,128,128]{3,2,1,0:T(8,128)(2,1)S(1)}, u32[]{:S(2)}, u32[]{:S(2)}) collective-permute-start(bf16[4,1,128,128]{3,2,1,0:T(8,128)(2,1)S(1)} %get-tuple-element.8), channel_id=1, source_target_pairs={{0,1},{1,2},{2,3},{4,5},{5,6},{6,7},{8,9},{9,10},{10,11},{12,13},{... | collective-permute-start | bytes 393224 | tf_op jit(solution)/shard_map/ppermute | solution.py:18
  15.9 1.3 collective-permute-start.3
  17.2 10.7 %collective-permute-done.3.edges_ref = bf16[2,2,128,128]{3,2,1,0:T(8,128)(2,1)S(1)} collective-permute-done((bf16[2,2,128,128]{3,2,1,0:T(8,128)(2,1)S(1)}, bf16[2,2,128,128]{3,2,1,0:T(8,128)(2,1)S(1)}, u32[]{:S(2)}, u32[]{:S(2)}) %collective-permute-start.3) | collective-permute-done | bytes 131104 | tf_op jit(solution)/shard_map/ppermute | solution.py:18
  29.4 9.1 %wsum.3 = f32[3456,128]{1,0:T(8,128)} custom-call(bf16[4,8,128,128]{3,2,1,0:T(8,128)(2,1)} %grad_ref.3, bf16[4,1,128,128]{3,2,1,0:T(8,128)(2,1)} %copy-done.3, bf16[4,1,128,128]{3,2,1,0:T(8,128)(2,1)} %copy-done.2, bf16[2,8,128,128]{3,2,1,0:T(8,128)(2,1)} %copy-done.5, bf16[2,2,128,128]{3,2,1,0:T(8,128)(2,1)} %copy-done.7, bf16[4,8,128,128]{3,2,1,0:T(8,128)(2,1)} %saved_ref.7), custom_call_target="tpu_custom_call" | custom-call | flops 3623878656 | bytes 2097152 | tf_op jit(solution)/shard_map/wsum/pallas_call | solution.py:142
  38.5 1.5 reshape.20
  40.0 2.3 %copy.14 = f32[8,4,108,128]{3,0,2,1:T(8,128)} copy(f32[8,4,108,128]{3,2,1,0:T(8,128)S(1)} %reshape.20) | data formatting | bytes 3538944 | tf_op jit(solution)/shard_map/reshape | solution.py:163
  42.3 11.1 %spread.2.grad_ref = bf16[4,8,128,128]{3,2,1,0:T(8,128)(2,1)} custom-call(bf16[4,8,128,128]{3,2,1,0:T(8,128)(2,1)} %grad_ref.3, bf16[4,1,128,128]{3,2,1,0:T(8,128)(2,1)} %copy-done.3, bf16[4,1,128,128]{3,2,1,0:T(8,128)(2,1)} %copy-done.2, bf16[2,8,128,128]{3,2,1,0:T(8,128)(2,1)} %copy-done.5, bf16[2,2,128,128]{3,2,1,0:T(8,128)(2,1)} %copy-done.7, ...), custom_call_target="tpu_custom_call" | custom-call | flops 4831838208 | bytes 2097152 | tf_op jit(solution)/shard_map/spread/pallas_call | solution.py:124
  54.5 1.3 collective-permute-start.6
  56.8 1.3 collective-permute-start.5
  58.1 3.2 %collective-permute-start.4 = (bf16[4,1,128,128]{3,2,1,0:T(8,128)(2,1)S(1)}, bf16[4,1,128,128]{3,2,1,0:T(8,128)(2,1)S(1)}, u32[]{:S(2)}, u32[]{:S(2)}) collective-permute-start(bf16[4,1,128,128]{3,2,1,0:T(8,128)(2,1)S(1)} %get-tuple-element.6), channel_id=1, source_target_pairs={{0,1},{1,2},{2,3},{4,5},{5,6},{6,7},{8,9},{9,10},{10,11},{12,13},{... | collective-permute-start | bytes 393224 | tf_op jit(solution)/shard_map/ppermute | solution.py:18
  62.4 1.3 collective-permute-start.7
  63.7 8.8 %collective-permute-done.7.edges_ref = bf16[2,2,128,128]{3,2,1,0:T(8,128)(2,1)S(1)} collective-permute-done((bf16[2,2,128,128]{3,2,1,0:T(8,128)(2,1)S(1)}, bf16[2,2,128,128]{3,2,1,0:T(8,128)(2,1)S(1)}, u32[]{:S(2)}, u32[]{:S(2)}) %collective-permute-start.7) | collective-permute-done | bytes 131104 | tf_op jit(solution)/shard_map/ppermute | solution.py:18
  73.9 9.1 %wsum.2 = f32[3456,128]{1,0:T(8,128)} custom-call(bf16[4,8,128,128]{3,2,1,0:T(8,128)(2,1)} %spread.2.grad_ref, bf16[4,1,128,128]{3,2,1,0:T(8,128)(2,1)} %copy-done.1, bf16[4,1,128,128]{3,2,1,0:T(8,128)(2,1)} %copy-done, bf16[2,8,128,128]{3,2,1,0:T(8,128)(2,1)} %copy-done.4, bf16[2,2,128,128]{3,2,1,0:T(8,128)(2,1)} %copy-done.6, ...), custom_call_target="tpu_custom_call" | custom-call | flops 3623878656 | bytes 2097152 | tf_op jit(solution)/shard_map/wsum/pallas_call | solution.py:142
  83.0 1.5 reshape.18
  84.5 2.3 %copy.12 = f32[8,4,108,128]{3,0,2,1:T(8,128)} copy(f32[8,4,108,128]{3,2,1,0:T(8,128)S(1)} %reshape.18) | data formatting | bytes 3538944 | tf_op jit(solution)/shard_map/reshape | solution.py:163
  86.8 35.5 %reduce-scatter.5.cloned.1.call-done = f32[8,1,108,128]{3,0,2,1:T(8,128)} async-done(((f32[8,4,108,128]{3,0,2,1:T(8,128)}), f32[8,1,108,128]{3,0,2,1:T(8,128)}) %reduce-scatter.5.cloned.1.call-update) | async-done | bytes 442384 | tf_op jit(solution)/shard_map/reduce_scatter | solution.py:164
  122.9 11.1 %spread.3 = bf16[4,8,128,128]{3,2,1,0:T(8,128)(2,1)} custom-call(bf16[4,8,128,128]{3,2,1,0:T(8,128)(2,1)} %spread.2.grad_ref, bf16[4,1,128,128]{3,2,1,0:T(8,128)(2,1)} %copy-done.1, bf16[4,1,128,128]{3,2,1,0:T(8,128)(2,1)} %copy-done, bf16[2,8,128,128]{3,2,1,0:T(8,128)(2,1)} %copy-done.4, bf16[2,2,128,128]{3,2,1,0:T(8,128)(2,1)} %copy-done.6, ...), custom_call_target="tpu_custom_call" | custom-call | flops 4831838208 | bytes 2097152 | tf_op jit(solution)/shard_map/spread/pallas_call | solution.py:124
  134.1 68.2 %all-reduce.5.cloned.1.call-done = (f32[8,1,108,128]{3,0,2,1:T(8,128)}, f32[8,1,108,128]{3,0,2,1:T(8,128)}) async-done(((f32[8,1,108,128]{3,0,2,1:T(8,128)}, f32[8,1,108,128]{3,0,2,1:T(8,128)}), (f32[8,1,108,128]{3,0,2,1:T(8,128)}, f32[8,1,108,128]{3,0,2,1:T(8,128)})) %all-reduce.5.cloned.1.call-update) | async-done | bytes 884752
  202.2 1.6 dynamic-slice_bitcast_fusion.1
  203.8 1.6 dynamic-slice_bitcast_fusion
  205.5 5.7 %all-gather.1 = f32[1,1,432,128]{3,1,0,2:T(1,128)S(1)} all-gather(f32[1,1,108,128]{3,1,0,2:T(1,128)S(1)} %dynamic-slice_bitcast_fusion), channel_id=3, replica_groups=mesh['tm'=8,'rows'=4] {'rows'}, dimensions={2}, use_global_device_ids=true | all-gather | bytes 276480 | tf_op jit(solution)/shard_map/all_gather | solution.py:166
  212.0 5.7 %all-gather = f32[1,1,432,128]{3,1,0,2:T(1,128)S(1)} all-gather(f32[1,1,108,128]{3,1,0,2:T(1,128)S(1)} %dynamic-slice_bitcast_fusion.1), channel_id=2, replica_groups=mesh['tm'=8,'rows'=4] {'rows'}, dimensions={2}, use_global_device_ids=true | all-gather | bytes 276480 | tf_op jit(solution)/shard_map/all_gather | solution.py:166
  (44 shorter events, 11.5 us)
Async XLA Ops:
  7.2 79.7 %reduce-scatter.7.cloned.1.call-start = ((), (), s32[]{:S(2)}) async-start(), calls=%async_computation.3 | async-start | bytes 2211840 | tf_op jit(solution)/shard_map/reduce_scatter | solution.py:164
  8.3 19.6 %collective-permute-start.2 = (bf16[2,8,128,128]{3,2,1,0:T(8,128)(2,1)S(1)}, bf16[2,8,128,128]{3,2,1,0:T(8,128)(2,1)S(1)}, u32[]{:S(2)}, u32[]{:S(2)}) collective-permute-start(bf16[2,8,128,128]{3,2,1,0:T(8,128)(2,1)S(1)} %slice.32), channel_id=1, source_target_pairs={{4,0},{8,4},{12,8},{16,12},{20,16},{24,20},{28,24},{5,1},{9,5},{13... | collective-permute-start | bytes 1572872 | tf_op jit(solution)/shard_map/ppermute | solution.py:18
  10.6 4.3 %collective-permute-start.1 = (bf16[4,1,128,128]{3,2,1,0:T(8,128)(2,1)S(1)}, bf16[4,1,128,128]{3,2,1,0:T(8,128)(2,1)S(1)}, u32[]{:S(2)}, u32[]{:S(2)}) collective-permute-start(bf16[4,1,128,128]{3,2,1,0:T(8,128)(2,1)S(1)} %get-tuple-element.7), channel_id=1, source_target_pairs={{1,0},{2,1},{3,2},{5,4},{6,5},{7,6},{9,8},{10,9},{11,10},{13,12},{... | collective-permute-start | bytes 393224 | tf_op jit(solution)/shard_map/ppermute | solution.py:18
  11.9 4.0 %collective-permute-start = (bf16[4,1,128,128]{3,2,1,0:T(8,128)(2,1)S(1)}, bf16[4,1,128,128]{3,2,1,0:T(8,128)(2,1)S(1)}, u32[]{:S(2)}, u32[]{:S(2)}) collective-permute-start(bf16[4,1,128,128]{3,2,1,0:T(8,128)(2,1)S(1)} %get-tuple-element.8), channel_id=1, source_target_pairs={{0,1},{1,2},{2,3},{4,5},{5,6},{6,7},{8,9},{9,10},{10,11},{12,13},{... | collective-permute-start | bytes 393224 | tf_op jit(solution)/shard_map/ppermute | solution.py:18
  14.9 13.0 %copy-start.2 = (bf16[4,1,128,128]{3,2,1,0:T(8,128)(2,1)}, bf16[4,1,128,128]{3,2,1,0:T(8,128)(2,1)S(1)}, u32[]{:S(2)}) copy-start(bf16[4,1,128,128]{3,2,1,0:T(8,128)(2,1)S(1)} %collective-permute-done.1.below_ref) | copy-start | bytes 393220
  15.9 12.0 %copy-start.3 = (bf16[4,1,128,128]{3,2,1,0:T(8,128)(2,1)}, bf16[4,1,128,128]{3,2,1,0:T(8,128)(2,1)S(1)}, u32[]{:S(2)}) copy-start(bf16[4,1,128,128]{3,2,1,0:T(8,128)(2,1)S(1)} %collective-permute-done.above_ref) | copy-start | bytes 393220
  15.9 12.0 %collective-permute-start.3 = (bf16[2,2,128,128]{3,2,1,0:T(8,128)(2,1)S(1)}, bf16[2,2,128,128]{3,2,1,0:T(8,128)(2,1)S(1)}, u32[]{:S(2)}, u32[]{:S(2)}) collective-permute-start(bf16[2,2,128,128]{3,2,1,0:T(8,128)(2,1)S(1)} %pad_maximum_fusion), channel_id=1, source_target_pairs={{4,0},{8,4},{12,8},{16,12},{20,16},{24,20},{28,24},{5,1},{9,5},{13... | collective-permute-start | bytes 393224 | tf_op jit(solution)/shard_map/ppermute | solution.py:18
  27.9 0.7 copy-start.7
  28.6 0.8 copy-start.5
  42.3 80.1 %reduce-scatter.5.cloned.1.call-start = ((), (), s32[]{:S(2)}) async-start(), calls=%async_computation.2 | async-start | bytes 2211840 | tf_op jit(solution)/shard_map/reduce_scatter | solution.py:164
  54.5 17.9 %collective-permute-start.6 = (bf16[2,8,128,128]{3,2,1,0:T(8,128)(2,1)S(1)}, bf16[2,8,128,128]{3,2,1,0:T(8,128)(2,1)S(1)}, u32[]{:S(2)}, u32[]{:S(2)}) collective-permute-start(bf16[2,8,128,128]{3,2,1,0:T(8,128)(2,1)S(1)} %slice.44), channel_id=1, source_target_pairs={{4,0},{8,4},{12,8},{16,12},{20,16},{24,20},{28,24},{5,1},{9,5},{13... | collective-permute-start | bytes 1572872 | tf_op jit(solution)/shard_map/ppermute | solution.py:18
  56.8 4.5 %collective-permute-start.5 = (bf16[4,1,128,128]{3,2,1,0:T(8,128)(2,1)S(1)}, bf16[4,1,128,128]{3,2,1,0:T(8,128)(2,1)S(1)}, u32[]{:S(2)}, u32[]{:S(2)}) collective-permute-start(bf16[4,1,128,128]{3,2,1,0:T(8,128)(2,1)S(1)} %get-tuple-element.5), channel_id=1, source_target_pairs={{1,0},{2,1},{3,2},{5,4},{6,5},{7,6},{9,8},{10,9},{11,10},{13,12},{... | collective-permute-start | bytes 393224 | tf_op jit(solution)/shard_map/ppermute | solution.py:18
  58.1 4.2 %collective-permute-start.4 = (bf16[4,1,128,128]{3,2,1,0:T(8,128)(2,1)S(1)}, bf16[4,1,128,128]{3,2,1,0:T(8,128)(2,1)S(1)}, u32[]{:S(2)}, u32[]{:S(2)}) collective-permute-start(bf16[4,1,128,128]{3,2,1,0:T(8,128)(2,1)S(1)} %get-tuple-element.6), channel_id=1, source_target_pairs={{0,1},{1,2},{2,3},{4,5},{5,6},{6,7},{8,9},{9,10},{10,11},{12,13},{... | collective-permute-start | bytes 393224 | tf_op jit(solution)/shard_map/ppermute | solution.py:18
  61.4 11.1 %copy-start = (bf16[4,1,128,128]{3,2,1,0:T(8,128)(2,1)}, bf16[4,1,128,128]{3,2,1,0:T(8,128)(2,1)S(1)}, u32[]{:S(2)}) copy-start(bf16[4,1,128,128]{3,2,1,0:T(8,128)(2,1)S(1)} %collective-permute-done.5.below_ref) | copy-start | bytes 393220
  62.3 10.1 %copy-start.1 = (bf16[4,1,128,128]{3,2,1,0:T(8,128)(2,1)}, bf16[4,1,128,128]{3,2,1,0:T(8,128)(2,1)S(1)}, u32[]{:S(2)}) copy-start(bf16[4,1,128,128]{3,2,1,0:T(8,128)(2,1)S(1)} %collective-permute-done.4.above_ref) | copy-start | bytes 393220
  62.4 10.1 %collective-permute-start.7 = (bf16[2,2,128,128]{3,2,1,0:T(8,128)(2,1)S(1)}, bf16[2,2,128,128]{3,2,1,0:T(8,128)(2,1)S(1)}, u32[]{:S(2)}, u32[]{:S(2)}) collective-permute-start(bf16[2,2,128,128]{3,2,1,0:T(8,128)(2,1)S(1)} %pad_maximum_fusion.1), channel_id=1, source_target_pairs={{4,0},{8,4},{12,8},{16,12},{20,16},{24,20},{28,24},{5,1},{9,5},{13... | collective-permute-start | bytes 393224 | tf_op jit(solution)/shard_map/ppermute | solution.py:18
  72.4 0.7 copy-start.6
  73.1 0.8 copy-start.4
  86.7 35.6 %copy-start.8 = (u32[32]{0:T(128)S(1)}, u32[32]{0:T(128)}, u32[]{:S(2)}) copy-start(u32[32]{0:T(128)} %constant.7) | copy-start | bytes 388
  86.7 115.5 %all-reduce.5.cloned.1.call-start = ((), (), s32[]{:S(2)}) async-start(), calls=%async_computation.4 | async-start | bytes 1769472
Sparse Core Ops, SparseCore 0:
  42.4 31.6 reduce-scatter.6
  86.9 35.4 reduce-scatter.4
  125.8 76.3 all-reduce.4

commit v2 on v1

--- a/solution.py
+++ b/solution.py
@@ -154,16 +154,25 @@
     )(*pieces, saved)
 
 
-def reduced(wsum):
-    depth, chans = wsum.shape
+def exchanged_sum(parts, axis, dim):
+    return jnp.sum(lax.all_to_all(parts, axis, split_axis=dim, concat_axis=dim, tiled=True), axis=dim)
+
+
+def reduced(wsum_first, wsum_second, factor):
+    depth, chans = wsum_first.shape
     slots, bands = lax.axis_size("tm"), lax.axis_size("rows")
     share = depth // slots
     if share % bands:
-        return lax.psum_scatter(lax.psum(wsum, "rows"), "tm", scatter_dimension=0, tiled=True)
-    parts = wsum.reshape(slots, bands, share // bands, chans)
-    banded = lax.psum_scatter(parts, "rows", scatter_dimension=1, tiled=True)
-    mine = lax.psum_scatter(banded, "tm", scatter_dimension=0, tiled=True)
-    return lax.all_gather(mine.reshape(share // bands, chans), "rows", axis=0, tiled=True)
+        first, second = lax.psum((wsum_first, wsum_second), "rows")
+        both = jnp.stack([first.reshape(slots, share, chans), second.reshape(slots, share, chans)], axis=1)
+        mine = exchanged_sum(both, "tm", 0) * factor
+        return mine[0], mine[1]
+    split = (slots, bands, share // bands, chans)
+    second = lax.psum_scatter(wsum_second.reshape(split), "rows", scatter_dimension=1, tiled=False)
+    first = exchanged_sum(wsum_first.reshape(split), "rows", 1)
+    mine = exchanged_sum(jnp.stack([first, second], axis=1), "tm", 0) * factor
+    whole = lax.all_gather(mine, "rows", axis=1, tiled=True)
+    return whole[0], whole[1]
 
 
 def body(upstream, saved_first, saved_second, weight_first, weight_second):
@@ -175,7 +184,7 @@
     wsum_first = wsum_of(pieces_mid, saved_first)
     frames, height, width, chans = upstream.shape
     factor = 1.0 / math.sqrt(frames * lax.axis_size("tm") * height * lax.axis_size("rows") * width)
-    return (grad_input, reduced(wsum_first) * factor, reduced(wsum_second) * factor)
+    return (grad_input, *reduced(wsum_first, wsum_second, factor))
 
 
 def solution(mesh):

time: 226 us -> 161 us (0.71)
  waiting for transfers between devices: 125 us -> 32.6 us
  blocking collectives: 11.3 us -> 34.9 us
  starting transfers between devices: 14.1 us -> 20.8 us
  local copies, waits for them, and re-layouts: 18.4 us -> 16 us
    unnamed x4 -> x1, waiting for transfers between devices: 68.2 us -> 0.02 us
    reduce_scatter x2 -> x1, waiting for transfers between devices: 35.5 us -> 0.02 us  [reduced(): lax.psum_scatter(wsum_second.reshape(split), 'rows', scatter_dimension=1,...]
    all_to_all x0 -> x1, blocking collectives: none -> 28.6 us  [exchanged_sum(): lax.all_to_all(parts, axis, split_axis=dim, concat_axis=dim, tiled=True)]
    all_to_all x0 -> x1, waiting for transfers between devices: none -> 11.2 us  [exchanged_sum(): lax.all_to_all(parts, axis, split_axis=dim, concat_axis=dim, tiled=True)]
    all_to_all x0 -> x1, starting transfers between devices: none -> 6.77 us  [exchanged_sum(): lax.all_to_all(parts, axis, split_axis=dim, concat_axis=dim, tiled=True)]
    all_gather x2 -> x1, blocking collectives: 11.3 us -> 6.28 us  [reduced(): whole = lax.all_gather(mine, 'rows', axis=1, tiled=True)]
    reduce_scatter x2 -> x0, local copies, waits for them, and re-layouts: 3.24 us -> none  [reduced(): mine = lax.psum_scatter(banded, 'tm', scatter_dimension=0, tiled=True)]
  transfers between devices with their start and end apart: 11 -> 10, of which waited for: 6 -> 5; matrix products, arithmetic and copies ran while one was open for 3% -> 4% of each run, Pallas kernels for 14% -> 20%
where the time goes in v2:
time: 161 us
  Pallas kernels  40.5 us (25%)
  blocking collectives  34.9 us (22%)
  waiting for transfers between devices  32.6 us (20%)
  starting transfers between devices  20.8 us (13%)
  local copies, waits for them, and re-layouts  16 us (10%)
  between operations  14.2 us (9%)
  other arithmetic  1.62 us (1%)
    all_to_all x1, blocking collectives, exchanged_sum(): lax.all_to_all(parts, axis, split_axis=dim, concat_axis=dim, tiled=True)  28.6 us
    pallas_call x2, Pallas kernels, spread_of(): pl.pallas_call(spread_kernel, out_shape=jax.ShapeDtypeStruct(saved.shape,...  22.3 us
    ppermute x8, waiting for transfers between devices, shifted(): return lax.ppermute(block, axis, route)  21.3 us
    pallas_call x2, Pallas kernels, wsum_of(): pl.pallas_call(wsum_kernel, out_shape=jax.ShapeDtypeStruct((27 * chans, c...  18.2 us
    ppermute x8, starting transfers between devices, shifted(): return lax.ppermute(block, axis, route)  14 us
    all_to_all x1, waiting for transfers between devices, exchanged_sum(): lax.all_to_all(parts, axis, split_axis=dim, concat_axis=dim, tiled=True)  11.2 us
    all_to_all x1, starting transfers between devices, exchanged_sum(): lax.all_to_all(parts, axis, split_axis=dim, concat_axis=dim, tiled=True)  6.77 us
    all_gather x1, blocking collectives, reduced(): whole = lax.all_gather(mine, 'rows', axis=1, tiled=True)  6.28 us
  transfers between devices with their start and end apart: 10, of which 5 were waited for; matrix products, arithmetic and copies ran while one was open for 4% of the time, Pallas kernels for 20%

profile of v2, /device:TPU:0, one launch (start us, length us, event | category | flops | bytes accessed | tf_op | source)
XLA Modules:
  0.0 160.6 jit_solution(7852985638606203349)
XLA Ops:
  7.2 1.1 slice.38
  8.3 1.3 collective-permute-start.2
  10.6 1.3 collective-permute-start.1
  11.9 3.0 %collective-permute-start = (bf16[4,1,128,128]{3,2,1,0:T(8,128)(2,1)S(1)}, bf16[4,1,128,128]{3,2,1,0:T(8,128)(2,1)S(1)}, u32[]{:S(2)}, u32[]{:S(2)}) collective-permute-start(bf16[4,1,128,128]{3,2,1,0:T(8,128)(2,1)S(1)} %get-tuple-element.6), channel_id=1, source_target_pairs={{0,1},{1,2},{2,3},{4,5},{5,6},{6,7},{8,9},{9,10},{10,11},{12,13},{... | collective-permute-start | bytes 393224 | tf_op jit(solution)/shard_map/ppermute | solution.py:18
  15.9 1.3 collective-permute-start.3
  17.2 10.7 %collective-permute-done.3.edges_ref = bf16[2,2,128,128]{3,2,1,0:T(8,128)(2,1)S(1)} collective-permute-done((bf16[2,2,128,128]{3,2,1,0:T(8,128)(2,1)S(1)}, bf16[2,2,128,128]{3,2,1,0:T(8,128)(2,1)S(1)}, u32[]{:S(2)}, u32[]{:S(2)}) %collective-permute-start.3) | collective-permute-done | bytes 131104 | tf_op jit(solution)/shard_map/ppermute | solution.py:18
  29.4 9.1 %wsum.3 = f32[3456,128]{1,0:T(8,128)} custom-call(bf16[4,8,128,128]{3,2,1,0:T(8,128)(2,1)} %grad_ref.3, bf16[4,1,128,128]{3,2,1,0:T(8,128)(2,1)} %copy-done.3, bf16[4,1,128,128]{3,2,1,0:T(8,128)(2,1)} %copy-done.2, bf16[2,8,128,128]{3,2,1,0:T(8,128)(2,1)} %copy-done.5, bf16[2,2,128,128]{3,2,1,0:T(8,128)(2,1)} %copy-done.7, bf16[4,8,128,128]{3,2,1,0:T(8,128)(2,1)} %saved_ref.7), custom_call_target="tpu_custom_call" | custom-call | flops 3623878656 | bytes 2097152 | tf_op jit(solution)/shard_map/wsum/pallas_call | solution.py:142
  38.5 1.5 reshape.13
  40.0 2.3 %copy.9 = f32[8,4,108,128]{3,0,2,1:T(8,128)} copy(f32[8,4,108,128]{3,2,1,0:T(8,128)S(1)} %reshape.13) | data formatting | bytes 3538944 | tf_op jit(solution)/shard_map/reshape | solution.py:171
  42.3 11.1 %spread.2.grad_ref = bf16[4,8,128,128]{3,2,1,0:T(8,128)(2,1)} custom-call(bf16[4,8,128,128]{3,2,1,0:T(8,128)(2,1)} %grad_ref.3, bf16[4,1,128,128]{3,2,1,0:T(8,128)(2,1)} %copy-done.3, bf16[4,1,128,128]{3,2,1,0:T(8,128)(2,1)} %copy-done.2, bf16[2,8,128,128]{3,2,1,0:T(8,128)(2,1)} %copy-done.5, bf16[2,2,128,128]{3,2,1,0:T(8,128)(2,1)} %copy-done.7, ...), custom_call_target="tpu_custom_call" | custom-call | flops 4831838208 | bytes 2097152 | tf_op jit(solution)/shard_map/spread/pallas_call | solution.py:124
  54.5 1.3 collective-permute-start.6
  56.8 1.3 collective-permute-start.5
  58.1 3.2 %collective-permute-start.4 = (bf16[4,1,128,128]{3,2,1,0:T(8,128)(2,1)S(1)}, bf16[4,1,128,128]{3,2,1,0:T(8,128)(2,1)S(1)}, u32[]{:S(2)}, u32[]{:S(2)}) collective-permute-start(bf16[4,1,128,128]{3,2,1,0:T(8,128)(2,1)S(1)} %get-tuple-element.4), channel_id=1, source_target_pairs={{0,1},{1,2},{2,3},{4,5},{5,6},{6,7},{8,9},{9,10},{10,11},{12,13},{... | collective-permute-start | bytes 393224 | tf_op jit(solution)/shard_map/ppermute | solution.py:18
  62.1 1.3 collective-permute-start.7
  63.4 9.0 %collective-permute-done.7.edges_ref = bf16[2,2,128,128]{3,2,1,0:T(8,128)(2,1)S(1)} collective-permute-done((bf16[2,2,128,128]{3,2,1,0:T(8,128)(2,1)S(1)}, bf16[2,2,128,128]{3,2,1,0:T(8,128)(2,1)S(1)}, u32[]{:S(2)}, u32[]{:S(2)}) %collective-permute-start.7) | collective-permute-done | bytes 131104 | tf_op jit(solution)/shard_map/ppermute | solution.py:18
  73.8 9.1 %wsum.2 = f32[3456,128]{1,0:T(8,128)} custom-call(bf16[4,8,128,128]{3,2,1,0:T(8,128)(2,1)} %spread.2.grad_ref, bf16[4,1,128,128]{3,2,1,0:T(8,128)(2,1)} %copy-done.1, bf16[4,1,128,128]{3,2,1,0:T(8,128)(2,1)} %copy-done, bf16[2,8,128,128]{3,2,1,0:T(8,128)(2,1)} %copy-done.4, bf16[2,2,128,128]{3,2,1,0:T(8,128)(2,1)} %copy-done.6, ...), custom_call_target="tpu_custom_call" | custom-call | flops 3623878656 | bytes 2097152 | tf_op jit(solution)/shard_map/wsum/pallas_call | solution.py:142
  82.9 1.5 reshape.12
  85.4 28.6 %all_to_all.10 = f32[8,4,108,128]{3,0,2,1:T(8,128)S(1)} all-to-all(f32[8,4,108,128]{3,0,2,1:T(8,128)S(1)} %copy.8), channel_id=1, replica_groups=mesh['tm'=8,'rows'=4] {'rows'}, dimensions={1} | all-to-all | bytes 3538944 | tf_op jit(solution)/shard_map/all_to_all | solution.py:158
  115.3 1.6 copy.10
  116.9 6.8 %all-to-all-start.1 = ((f32[8,2,108,128]{3,1,2,0:T(2,128)}), f32[8,2,108,128]{3,1,2,0:T(2,128)S(1)}, u32[]{:S(2)}, u32[]{:S(2)}) async-start(f32[8,2,108,128]{3,1,2,0:T(2,128)} %copy.10), calls=%async_computation.2 | async-start | bytes 1769472 | tf_op jit(solution)/shard_map/all_to_all | solution.py:158
  123.6 11.1 %spread.3 = bf16[4,8,128,128]{3,2,1,0:T(8,128)(2,1)} custom-call(bf16[4,8,128,128]{3,2,1,0:T(8,128)(2,1)} %spread.2.grad_ref, bf16[4,1,128,128]{3,2,1,0:T(8,128)(2,1)} %copy-done.1, bf16[4,1,128,128]{3,2,1,0:T(8,128)(2,1)} %copy-done, bf16[2,8,128,128]{3,2,1,0:T(8,128)(2,1)} %copy-done.4, bf16[2,2,128,128]{3,2,1,0:T(8,128)(2,1)} %copy-done.6, ...), custom_call_target="tpu_custom_call" | custom-call | flops 4831838208 | bytes 2097152 | tf_op jit(solution)/shard_map/spread/pallas_call | solution.py:124
  134.8 11.2 %all-to-all-done.1 = f32[8,2,108,128]{3,1,2,0:T(2,128)S(1)} async-done(((f32[8,2,108,128]{3,1,2,0:T(2,128)}), f32[8,2,108,128]{3,1,2,0:T(2,128)S(1)}, u32[]{:S(2)}, u32[]{:S(2)}) %all-to-all-start.1) | async-done | bytes 884768 | tf_op jit(solution)/shard_map/all_to_all | solution.py:158
  146.3 6.3 %all_gather.3 = f32[2,432,128]{2,0,1:T(2,128)S(1)} all-gather(f32[2,108,128]{2,0,1:T(2,128)S(1)} %broadcast_multiply_fusion), channel_id=1, replica_groups=mesh['tm'=8,'rows'=4] {'rows'}, dimensions={1}, use_global_device_ids=true | all-gather | bytes 552960 | tf_op jit(solution)/shard_map/all_gather | solution.py:174
  152.6 1.1 fusion.2
  (39 shorter events, 10.4 us)
Async XLA Ops:
  7.2 107.0 %reduce-scatter.2.cloned.1.call-start = ((), (), s32[]{:S(2)}) async-start(), calls=%async_computation.3 | async-start | bytes 2211840 | tf_op jit(solution)/shard_map/reduce_scatter | solution.py:171
  8.3 19.6 %collective-permute-start.2 = (bf16[2,8,128,128]{3,2,1,0:T(8,128)(2,1)S(1)}, bf16[2,8,128,128]{3,2,1,0:T(8,128)(2,1)S(1)}, u32[]{:S(2)}, u32[]{:S(2)}) collective-permute-start(bf16[2,8,128,128]{3,2,1,0:T(8,128)(2,1)S(1)} %slice.38), channel_id=1, source_target_pairs={{4,0},{8,4},{12,8},{16,12},{20,16},{24,20},{28,24},{5,1},{9,5},{13... | collective-permute-start | bytes 1572872 | tf_op jit(solution)/shard_map/ppermute | solution.py:18
  10.6 4.3 %collective-permute-start.1 = (bf16[4,1,128,128]{3,2,1,0:T(8,128)(2,1)S(1)}, bf16[4,1,128,128]{3,2,1,0:T(8,128)(2,1)S(1)}, u32[]{:S(2)}, u32[]{:S(2)}) collective-permute-start(bf16[4,1,128,128]{3,2,1,0:T(8,128)(2,1)S(1)} %get-tuple-element.5), channel_id=1, source_target_pairs={{1,0},{2,1},{3,2},{5,4},{6,5},{7,6},{9,8},{10,9},{11,10},{13,12},{... | collective-permute-start | bytes 393224 | tf_op jit(solution)/shard_map/ppermute | solution.py:18
  11.9 4.0 %collective-permute-start = (bf16[4,1,128,128]{3,2,1,0:T(8,128)(2,1)S(1)}, bf16[4,1,128,128]{3,2,1,0:T(8,128)(2,1)S(1)}, u32[]{:S(2)}, u32[]{:S(2)}) collective-permute-start(bf16[4,1,128,128]{3,2,1,0:T(8,128)(2,1)S(1)} %get-tuple-element.6), channel_id=1, source_target_pairs={{0,1},{1,2},{2,3},{4,5},{5,6},{6,7},{8,9},{9,10},{10,11},{12,13},{... | collective-permute-start | bytes 393224 | tf_op jit(solution)/shard_map/ppermute | solution.py:18
  14.9 13.0 %copy-start.2 = (bf16[4,1,128,128]{3,2,1,0:T(8,128)(2,1)}, bf16[4,1,128,128]{3,2,1,0:T(8,128)(2,1)S(1)}, u32[]{:S(2)}) copy-start(bf16[4,1,128,128]{3,2,1,0:T(8,128)(2,1)S(1)} %collective-permute-done.1.below_ref) | copy-start | bytes 393220
  15.9 12.0 %copy-start.3 = (bf16[4,1,128,128]{3,2,1,0:T(8,128)(2,1)}, bf16[4,1,128,128]{3,2,1,0:T(8,128)(2,1)S(1)}, u32[]{:S(2)}) copy-start(bf16[4,1,128,128]{3,2,1,0:T(8,128)(2,1)S(1)} %collective-permute-done.above_ref) | copy-start | bytes 393220
  15.9 12.0 %collective-permute-start.3 = (bf16[2,2,128,128]{3,2,1,0:T(8,128)(2,1)S(1)}, bf16[2,2,128,128]{3,2,1,0:T(8,128)(2,1)S(1)}, u32[]{:S(2)}, u32[]{:S(2)}) collective-permute-start(bf16[2,2,128,128]{3,2,1,0:T(8,128)(2,1)S(1)} %pad_maximum_fusion.1), channel_id=1, source_target_pairs={{4,0},{8,4},{12,8},{16,12},{20,16},{24,20},{28,24},{5,1},{9,5},{13... | collective-permute-start | bytes 393224 | tf_op jit(solution)/shard_map/ppermute | solution.py:18
  27.9 0.7 copy-start.7
  28.6 0.8 copy-start.5
  54.5 17.9 %collective-permute-start.6 = (bf16[2,8,128,128]{3,2,1,0:T(8,128)(2,1)S(1)}, bf16[2,8,128,128]{3,2,1,0:T(8,128)(2,1)S(1)}, u32[]{:S(2)}, u32[]{:S(2)}) collective-permute-start(bf16[2,8,128,128]{3,2,1,0:T(8,128)(2,1)S(1)} %slice.52), channel_id=1, source_target_pairs={{4,0},{8,4},{12,8},{16,12},{20,16},{24,20},{28,24},{5,1},{9,5},{13... | collective-permute-start | bytes 1572872 | tf_op jit(solution)/shard_map/ppermute | solution.py:18
  56.8 4.5 %collective-permute-start.5 = (bf16[4,1,128,128]{3,2,1,0:T(8,128)(2,1)S(1)}, bf16[4,1,128,128]{3,2,1,0:T(8,128)(2,1)S(1)}, u32[]{:S(2)}, u32[]{:S(2)}) collective-permute-start(bf16[4,1,128,128]{3,2,1,0:T(8,128)(2,1)S(1)} %get-tuple-element.3), channel_id=1, source_target_pairs={{1,0},{2,1},{3,2},{5,4},{6,5},{7,6},{9,8},{10,9},{11,10},{13,12},{... | collective-permute-start | bytes 393224 | tf_op jit(solution)/shard_map/ppermute | solution.py:18
  58.1 4.0 %collective-permute-start.4 = (bf16[4,1,128,128]{3,2,1,0:T(8,128)(2,1)S(1)}, bf16[4,1,128,128]{3,2,1,0:T(8,128)(2,1)S(1)}, u32[]{:S(2)}, u32[]{:S(2)}) collective-permute-start(bf16[4,1,128,128]{3,2,1,0:T(8,128)(2,1)S(1)} %get-tuple-element.4), channel_id=1, source_target_pairs={{0,1},{1,2},{2,3},{4,5},{5,6},{6,7},{8,9},{9,10},{10,11},{12,13},{... | collective-permute-start | bytes 393224 | tf_op jit(solution)/shard_map/ppermute | solution.py:18
  61.3 11.1 %copy-start = (bf16[4,1,128,128]{3,2,1,0:T(8,128)(2,1)}, bf16[4,1,128,128]{3,2,1,0:T(8,128)(2,1)S(1)}, u32[]{:S(2)}) copy-start(bf16[4,1,128,128]{3,2,1,0:T(8,128)(2,1)S(1)} %collective-permute-done.5.below_ref) | copy-start | bytes 393220
  62.1 10.3 %copy-start.1 = (bf16[4,1,128,128]{3,2,1,0:T(8,128)(2,1)}, bf16[4,1,128,128]{3,2,1,0:T(8,128)(2,1)S(1)}, u32[]{:S(2)}) copy-start(bf16[4,1,128,128]{3,2,1,0:T(8,128)(2,1)S(1)} %collective-permute-done.4.above_ref) | copy-start | bytes 393220
  62.1 10.3 %collective-permute-start.7 = (bf16[2,2,128,128]{3,2,1,0:T(8,128)(2,1)S(1)}, bf16[2,2,128,128]{3,2,1,0:T(8,128)(2,1)S(1)}, u32[]{:S(2)}, u32[]{:S(2)}) collective-permute-start(bf16[2,2,128,128]{3,2,1,0:T(8,128)(2,1)S(1)} %pad_maximum_fusion.2), channel_id=1, source_target_pairs={{4,0},{8,4},{12,8},{16,12},{20,16},{24,20},{28,24},{5,1},{9,5},{13... | collective-permute-start | bytes 393224 | tf_op jit(solution)/shard_map/ppermute | solution.py:18
  72.4 0.7 copy-start.6
  73.0 0.8 copy-start.4
  116.9 29.1 %all-to-all-start.1 = ((f32[8,2,108,128]{3,1,2,0:T(2,128)}), f32[8,2,108,128]{3,1,2,0:T(2,128)S(1)}, u32[]{:S(2)}, u32[]{:S(2)}) async-start(f32[8,2,108,128]{3,1,2,0:T(2,128)} %copy.10), calls=%async_computation.2 | async-start | bytes 1769472 | tf_op jit(solution)/shard_map/all_to_all | solution.py:158
Sparse Core Ops, SparseCore 0:
  42.4 31.5 reduce-scatter.1
